TPU v7x, 32 devices: a 4x4x1 block of a 4x4x8 slice. The times are simulated.
32 devices in a mesh: dp: 2 (over z, core), sp: 16 (over x, y).
Axes of the slice: x: 4, y: 4, z: 1, core: 2. Of those that a mesh axis runs over, the one named last changes fastest.
The devices are a block of a 4x4x8 slice.
Arguments:
- q: bfloat16 [64, 16, 128], P('dp'), parts along dimension 0
- k: bfloat16 [64, 8192, 16, 128], P('dp', 'sp'), parts along dimension 0
- v: bfloat16 [64, 8192, 16, 128], P('dp', 'sp'), parts along dimension 0
Outputs:
- q: bfloat16 [64, 16, 128], P('dp'), parts along dimension 0
There are 2 independent parts. A program takes and returns all parts, laid end to end along the dimension named above; each array names one.
All inputs are finite; a program needn't handle non-finite values.
Results may differ from a plain program's by a relative error of at most 0.012.
Values are sent between devices in bfloat16 or wider.
A program may use at most 768 MiB of HBM per device.

v0:
```python
import jax
import jax.numpy as jnp
from jax import lax
from jax.sharding import PartitionSpec as P


def einsum(form, a, b):
    return jnp.einsum(form, a.astype(jnp.float32), b.astype(jnp.float32))


def part_of(q, k, v):
    grouped = q.reshape(q.shape[0], k.shape[2], -1, q.shape[2])
    scores = einsum("bgsd,bugd->bgsu", grouped, k) * q.shape[2] ** -0.5
    high = jnp.max(scores, -1, keepdims=True)
    weights = jnp.exp(scores - high)
    seen = einsum("bgsu,bugd->bgsd", weights.astype(jnp.bfloat16), v)
    return jnp.concatenate([seen, jnp.sum(weights, -1, keepdims=True), high], -1)


def together(parts):
    seen, total, high = parts[..., :-2], parts[..., -2:-1], parts[..., -1:]
    scale = jnp.exp(high - jnp.max(high, 0))
    return (jnp.sum(seen * scale, 0) / jnp.sum(total * scale, 0)).astype(jnp.bfloat16)


def solution(mesh):
    def step(q, k, v):
        return together(lax.all_gather(part_of(q, k, v), "sp")).reshape(q.shape)

    return jax.shard_map(
        step,
        mesh=mesh,
        in_specs=(P("dp", None, None), P("dp", "sp", None, None), P("dp", "sp", None, None)),
        out_specs=P("dp", None, None),
        check_vma=False,
    )
```

profile of v0, /device:TPU:97, one launch (start us, length us, event | category | flops | bytes accessed | tf_op | source)
XLA Modules:
  0.0 167.9 jit_solution(2832112216813111622)
XLA Ops:
  6.5 0.0 all-gather.3.cloned.1.call-start
  6.6 31.9 %fusion.2 = f32[32,16,1,512]{3,2,1,0:T(1,128)S(1)} fusion(bf16[32,512,16,128]{3,2,1,0:T(8,128)(2,1)} %param.4, bf16[32,16,128,1]{2,1,0,3:T(8,128)(2,1)} %bitcast.25), kind=kOutput, calls=%fused_computation.2 | convolution fusion | flops 67108864 | bytes 68288512 | tf_op jit(solution)/shard_map/bgsd,bugd->bgsu/dot_general | solution.py:8
  38.5 0.2 fusion.9
  38.6 0.3 fusion.10
  39.0 0.3 copy.23
  39.2 0.3 copy.22
  39.5 32.6 %fusion = f32[32,16,1,128]{3,2,1,0:T(1,128)S(1)} fusion(bf16[32,512,16,128]{3,2,1,0:T(8,128)(2,1)} %param.5, bf16[32,16,512,1]{2,1,0,3:T(8,128)(2,1)S(1)} %get-tuple-element.7), kind=kOutput, calls=%fused_computation | convolution fusion | flops 67108864 | bytes 67895296 | tf_op jit(solution)/shard_map/bgsu,bugd->bgsd/dot_general | solution.py:8
  72.1 1.0 pad_maximum_fusion
  73.1 0.1 all-gather.3.cloned.1.call-update
  73.2 69.3 %all-gather.3.cloned.1.call-done = f32[512,16,1,130]{3,1,2,0:T(8,128)} async-done(((f32[32,16,1,130]{3,1,2,0:T(8,128)}), f32[512,16,1,130]{3,1,2,0:T(8,128)}) %all-gather.3.cloned.1.call-update) | async-done | bytes 4259856 | tf_op jit(solution)/shard_map/all_gather | solution.py:28
  142.4 3.4 %slice_reduce_fusion = f32[32,16]{1,0:T(8,128)S(1)} fusion(f32[16,32,16,1,130]{4,2,1,0,3:T(8,128)} %bitcast.21), kind=kLoop, calls=%fused_computation.9 | loop fusion | flops 7680 | bytes 34816 | tf_op jit(solution)/shard_map/reduce_max | solution.py:22
  145.9 6.7 %fusion.4 = (f32[32,16]{1,0:T(8,128)S(1)}, f32[16,32,16,1,1]{4,2,1,0,3:T(8,128)}) fusion(f32[16,32,16,1,130]{4,2,1,0,3:T(8,128)} %bitcast.22, f32[32,16]{1,0:T(8,128)S(1)} %slice_reduce_fusion), kind=kLoop, calls=%fused_computation.5 | loop fusion | flops 24064 | bytes 102400 | tf_op jit(solution)/shard_map/reduce_sum | solution.py:23
  152.5 4.7 %copy.36 = f32[16,32,16,1,1]{2,1,0,3,4:T(8,128)S(1)} copy(f32[16,32,16,1,1]{4,2,1,0,3:T(8,128)} %get-tuple-element.6) | data formatting | bytes 65536 | tf_op jit(solution)/shard_map/mul | solution.py:23
  157.3 2.9 %fusion.5 = f32[32,16,128]{2,1,0:T(8,128)S(1)} fusion(f32[16,32,16,1,130]{4,2,1,0,3:T(8,128)} %bitcast.23, f32[16,32,16]{2,1,0:T(8,128)S(1)} %bitcast.24), kind=kLoop, calls=%fused_computation.7 | loop fusion | flops 2031616 | bytes 4489216 | tf_op jit(solution)/shard_map/reduce_sum | solution.py:23
  160.2 0.8 divide_convert_fusion
Async XLA Ops:
  6.5 135.9 %all-gather.3.cloned.1.call-start = ((), (), s32[]{:S(2)}) async-start(), calls=%async_computation | async-start | bytes 8912896 | tf_op jit(solution)/shard_map/all_gather | solution.py:28
Sparse Core Ops, SparseCore 0:
  73.3 69.1 all-gather.2
where the time goes:
time: 168 us
  waiting for transfers between devices  69.3 us (41%)
  matrix products  64.5 us (38%)
  other arithmetic  15.3 us (9%)
  between operations  13.5 us (8%)
  local copies, waits for them, and re-layouts  5.22 us (3%)
    all_gather x1, waiting for transfers between devices, step(): return together(lax.all_gather(part_of(q, k, v), 'sp')).reshape(q.shape)  69.3 us
    dot_general x2, matrix products, einsum(): return jnp.einsum(form, a.astype(jnp.float32), b.astype(jnp.float32))  64.5 us
    reduce_sum x1, other arithmetic, together(): jnp.sum(total * scale, 0)  6.67 us
    mul x1, local copies, waits for them, and re-layouts, together(): seen * scale  4.69 us
    reduce_max x1, other arithmetic, together(): scale = jnp.exp(high - jnp.max(high, 0))  3.42 us
  transfers between devices with their start and end apart: 1, of which 1 were waited for; matrix products, arithmetic and copies ran while one was open for 0% of the time, Pallas kernels for 0%

commit v1 on v0

v1 whole, which is shorter than its diff:
```python
import functools

import jax
import jax.numpy as jnp
from jax import lax
from jax.experimental import pallas as pl
from jax.experimental.pallas import tpu as pltpu
from jax.sharding import PartitionSpec as P

SLOTS = 3
GROUP = 2
LAG = 4
TILE = 256
LOG2E = 1.4426950408889634


def attend(q, k, v, scores, scale):
    heads, head = q.shape
    rows = k.shape[0]
    half = rows // 2
    zero = jnp.zeros_like(q)
    twice = jnp.concatenate([jnp.concatenate([q, zero], 1), jnp.concatenate([zero, q], 1)], 0)
    shape = (2 * heads, TILE)
    own = lax.broadcasted_iota(jnp.int32, shape, 0) % heads == lax.broadcasted_iota(jnp.int32, shape, 1) % heads
    high = jnp.full(shape, -jnp.inf, jnp.float32)
    for i in range(half // TILE):
        keys = jnp.concatenate([k[pl.ds(i * TILE, TILE), :], k[pl.ds(half + i * TILE, TILE), :]], 1)
        s = lax.dot_general(twice, keys, (((1,), (1,)), ((), ())), preferred_element_type=jnp.float32)
        s = jnp.where(own, s, -jnp.inf)
        scores[:, pl.ds(i * TILE, TILE)] = s
        high = jnp.maximum(high, s)
    top = jnp.max(high, 1, keepdims=True)
    top = jnp.maximum(top[:heads], top[heads:])
    both = jnp.concatenate([top, top], 0)
    total = jnp.zeros(shape, jnp.float32)
    seen = jnp.zeros((2 * heads, 2 * head), jnp.float32)
    for i in range(half // TILE):
        w = jnp.exp2((scores[:, pl.ds(i * TILE, TILE)] - both) * (scale * LOG2E))
        total = total + w
        values = jnp.concatenate([v[pl.ds(i * TILE, TILE), :], v[pl.ds(half + i * TILE, TILE), :]], 1)
        seen = seen + jnp.dot(w.astype(jnp.bfloat16), values, preferred_element_type=jnp.float32)
    total = jnp.sum(total, 1, keepdims=True)
    return seen[:heads, :head] + seen[heads:, head:], top, total[:heads] + total[heads:]


def kernel(
    n, scale, q_ref, k_ref, v_ref, out_ref, k_buf, v_buf, scores_a, scores_b, parts, stats, k_sem, v_sem, send_sem, recv_sem, stat_send_sem, stat_recv_sem
):
    me = lax.axis_index("sp")
    sequences, heads, head = q_ref.shape
    groups = sequences // GROUP
    lanes = lax.broadcasted_iota(jnp.int32, (8, 128), 1)

    def fetch(g, start):
        slot = lax.rem(g, SLOTS)
        for hbm, buf, sem in ((k_ref, k_buf, k_sem), (v_ref, v_buf, v_sem)):
            for j in range(GROUP):
                copy = pltpu.make_async_copy(hbm.at[g * GROUP + j], buf.at[slot, j], sem.at[slot, j])
                copy.start() if start else copy.wait()

    for g in range(SLOTS):
        fetch(g, True)

    barrier = pltpu.get_barrier_semaphore()
    for d in range(1, n):
        pl.semaphore_signal(barrier, inc=1, device_id={"sp": lax.rem(me + d, n)}, device_id_type=pl.DeviceIdType.MESH)

    def send(g):
        @pl.loop(1, n)
        def _(d):
            peer = {"sp": lax.rem(me + d, n)}
            for buf, s_sem, r_sem in ((parts, send_sem, recv_sem), (stats, stat_send_sem, stat_recv_sem)):
                pltpu.make_async_remote_copy(
                    src_ref=buf.at[g, me], dst_ref=buf.at[g, me], send_sem=s_sem.at[g], recv_sem=r_sem.at[g], device_id=peer, device_id_type=pl.DeviceIdType.MESH
                ).start()

    def wait_all(buf, sem, g):
        whole = buf.at[g, pl.ds(0, n - 1)]
        pltpu.make_async_copy(whole, whole, sem.at[g]).wait()

    def combine(g):
        wait_all(parts, recv_sem, g)
        wait_all(stats, stat_recv_sem, g)
        stat = [stats[g, p] for p in range(n)]
        high = functools.reduce(jnp.maximum, stat)
        weight = [jnp.exp2((s - high) * (scale * LOG2E)) for s in stat]
        sums = [pltpu.roll(s, 126, 1) for s in stat]
        total = functools.reduce(jnp.add, [a * b for a, b in zip(weight, sums)])
        share = [w / total for w in weight]
        for j in range(GROUP):
            acc = [jnp.zeros((8, head), jnp.float32)] * 2
            for p in range(n):
                part = parts[g, p, j].astype(jnp.float32)
                for h in range(2):
                    lane = 4 * j + h
                    acc[h] = acc[h] + part[8 * h : 8 * h + 8] * share[p][:, lane : lane + 1]
            out_ref[g * GROUP + j] = jnp.concatenate(acc, 0).astype(out_ref.dtype)

    @pl.loop(0, groups)
    def _(g):
        slot = lax.rem(g, SLOTS)
        fetch(g, False)
        stat = jnp.zeros((8, 128), jnp.float32)
        for j, scores in enumerate((scores_a, scores_b)):
            seen, top, total = attend(q_ref[g * GROUP + j], k_buf.at[slot, j], v_buf.at[slot, j], scores, scale)
            parts[g, me, j] = seen.astype(parts.dtype)
            for lane, value in enumerate((top[:8], top[8:], total[:8], total[8:])):
                stat = jnp.where(lanes == 4 * j + lane, value, stat)
        stats[g, me] = stat

        @pl.when(g + SLOTS < groups)
        def _():
            fetch(g + SLOTS, True)

        @pl.when(g == 0)
        def _():
            pl.semaphore_wait(barrier, n - 1)

        send(g)

        @pl.when(g >= LAG)
        def _():
            combine(g - LAG)

    @pl.loop(groups - LAG, groups)
    def _(g):
        combine(g)

    @pl.loop(0, groups)
    def _(g):
        wait_all(parts, send_sem, g)
        wait_all(stats, stat_send_sem, g)


def solution(mesh):
    n = mesh.shape["sp"]

    def step(q, k, v):
        b, t, h, d = k.shape
        groups = b // GROUP
        return pl.pallas_call(
            functools.partial(kernel, n, d**-0.5),
            out_shape=jax.ShapeDtypeStruct(q.shape, q.dtype),
            in_specs=[pl.BlockSpec(memory_space=pltpu.VMEM), pl.BlockSpec(memory_space=pl.ANY), pl.BlockSpec(memory_space=pl.ANY)],
            out_specs=pl.BlockSpec(memory_space=pltpu.VMEM),
            scratch_shapes=[
                pltpu.VMEM((SLOTS, GROUP, t * h, d), k.dtype),
                pltpu.VMEM((SLOTS, GROUP, t * h, d), v.dtype),
                pltpu.VMEM((2 * h, t * h // 2), jnp.float32),
                pltpu.VMEM((2 * h, t * h // 2), jnp.float32),
                pltpu.VMEM((groups, n, GROUP, h, d), jnp.bfloat16),
                pltpu.VMEM((groups, n, 8, 128), jnp.float32),
                pltpu.SemaphoreType.DMA((SLOTS, GROUP)),
                pltpu.SemaphoreType.DMA((SLOTS, GROUP)),
                pltpu.SemaphoreType.DMA((groups,)),
                pltpu.SemaphoreType.DMA((groups,)),
                pltpu.SemaphoreType.DMA((groups,)),
                pltpu.SemaphoreType.DMA((groups,)),
            ],
            compiler_params=pltpu.CompilerParams(collective_id=0, has_side_effects=True, vmem_limit_bytes=60 * 2**20),
        )(q, k.reshape(b, t * h, d), v.reshape(b, t * h, d))

    return jax.shard_map(
        step,
        mesh=mesh,
        in_specs=(P("dp", None, None), P("dp", "sp", None, None), P("dp", "sp", None, None)),
        out_specs=P("dp", None, None),
        check_vma=False,
    )
```

time: 168 us -> 75.2 us (0.45)
  Pallas kernels: 0 us -> 73.5 us
  waiting for transfers between devices: 69.3 us -> 0 us
  matrix products: 64.5 us -> 0 us
  other arithmetic: 15.3 us -> 0 us
  between operations: 13.5 us -> 0.01 us
  local copies, waits for them, and re-layouts: 5.22 us -> 1.57 us
    pallas_call x0 -> x1, Pallas kernels: none -> 73.5 us  [step(): pl.pallas_call(functools.partial(kernel, n, d ** (-0.5)), out_shape=jax.S...]
    all_gather x1 -> x0, waiting for transfers between devices: 69.3 us -> none  [step(): return together(lax.all_gather(part_of(q, k, v), 'sp')).reshape(q.shape)]
    dot_general x2 -> x0, matrix products: 64.5 us -> none  [einsum(): return jnp.einsum(form, a.astype(jnp.float32), b.astype(jnp.float32))]
    reduce_sum x2 -> x0, other arithmetic: 9.61 us -> none  [the longest x1 6.67 us: together(): jnp.sum(total * scale, 0)]
    mul x1 -> x0, local copies, waits for them, and re-layouts: 4.69 us -> none  [together(): seen * scale]
    reduce_max x2 -> x0, other arithmetic: 3.6 us -> none  [the longest x1 3.42 us: together(): scale = jnp.exp(high - jnp.max(high, 0))]
  transfers between devices with their start and end apart: 1 -> 0, of which waited for: 1 -> 0; matrix products, arithmetic and copies ran while one was open for 0% -> 0% of each run, Pallas kernels for 0% -> 0%
where the time goes in v1:
time: 75.2 us; the launch traced here: 75.1 us
  Pallas kernels  73.5 us (98%)
  local copies, waits for them, and re-layouts  1.57 us (2%)
    pallas_call x1, Pallas kernels, step(): pl.pallas_call(functools.partial(kernel, n, d ** (-0.5)), out_shape=jax.S...  73.5 us
    unnamed x1, local copies, waits for them, and re-layouts  1.57 us

profile of v1, /device:TPU:97, one launch (start us, length us, event | category | flops | bytes accessed | tf_op | source)
XLA Modules:
  0.0 75.1 jit_solution(3036640794824426663)
XLA Ops:
  0.0 73.5 %shard_map.37 = bf16[32,16,128]{2,1,0:T(8,128)(2,1)} custom-call(bf16[32,16,128]{2,1,0:T(8,128)(2,1)} %q_ref.1, bf16[32,8192,128]{2,1,0:T(8,128)(2,1)} %bitcast.k_ref, bf16[32,8192,128]{2,1,0:T(8,128)(2,1)} %bitcast.1.v_ref), custom_call_target="tpu_custom_call" | custom-call | tf_op jit(solution)/shard_map/pallas_call | solution.py:141
  73.5 1.6 %copy.5 = bf16[32,16,128]{2,1,0:T(8,128)(2,1)} copy(bf16[32,16,128]{2,1,0:T(8,128)(2,1)} %shard_map.37) | data formatting | bytes 262144

commit v2 on v0

v2 whole, which is shorter than its diff:
```python
import functools

import jax
import jax.numpy as jnp
from jax import lax
from jax.experimental import pallas as pl
from jax.experimental.pallas import tpu as pltpu
from jax.sharding import PartitionSpec as P

SLOTS = 6
CHUNK = 4
LAST = (2, 1, 1)
BLOCK = 2
TILE = 256
LOG2E = 1.4426950408889634
SIDE = 4


def side_by_side(ref, i):
    half = ref.shape[0] // 2
    return jnp.concatenate([ref[pl.ds(i * TILE, TILE), :], ref[pl.ds(half + i * TILE, TILE), :]], 1)


def score(q, k, scores, result):
    heads = q.shape[0]
    zero = jnp.zeros_like(q)
    twice = jnp.concatenate([jnp.concatenate([q, zero], 1), jnp.concatenate([zero, q], 1)], 0)
    shape = (2 * heads, TILE)
    own = lax.broadcasted_iota(jnp.int32, shape, 0) % heads == lax.broadcasted_iota(jnp.int32, shape, 1) % heads
    high = jnp.full(shape, -jnp.inf, jnp.float32)
    for i in range(scores.shape[1] // TILE):
        s = lax.dot_general(twice, side_by_side(k, i), (((1,), (1,)), ((), ())), preferred_element_type=jnp.float32)
        s = jnp.where(own, s, -jnp.inf)
        scores[:, pl.ds(i * TILE, TILE)] = s
        high = jnp.maximum(high, s)
        yield
    top = jnp.max(high, 1, keepdims=True)
    top = jnp.maximum(top[:heads], top[heads:])
    result.append(jnp.concatenate([top, top], 0))


def weigh(scores, top, v, scale, result):
    heads, head = scores.shape[0] // 2, v.shape[1]
    total = jnp.zeros((2 * heads, TILE), jnp.float32)
    seen = jnp.zeros((2 * heads, 2 * head), jnp.float32)
    for i in range(scores.shape[1] // TILE):
        w = jnp.exp2((scores[:, pl.ds(i * TILE, TILE)] - top) * (scale * LOG2E))
        total = total + w
        seen = seen + jnp.dot(w.astype(jnp.bfloat16), side_by_side(v, i), preferred_element_type=jnp.float32)
        yield
    total = jnp.sum(total, 1, keepdims=True)
    result.extend((seen[:heads, :head] + seen[heads:, head:], total[:heads] + total[heads:]))


def together(*steps):
    live = list(steps)
    while live:
        live = [s for s in live if next(s, live) is not live]


def kernel(scale, q_ref, k_ref, v_ref, out_ref, k_buf, v_buf, scores_a, scores_b, tops, parts, stats, k_sem, v_sem, send_sem, recv_sem, stat_send_sem, stat_recv_sem):
    me = lax.axis_index("sp")
    place = (lax.div(me, SIDE), lax.rem(me, SIDE))
    sequences, heads, head = q_ref.shape
    chunks = sequences // CHUNK
    scores = (scores_a, scores_b)
    lanes = lax.broadcasted_iota(jnp.int32, (8, 128), 1)

    def key_copy(s):
        slot = lax.rem(s, SLOTS)
        return pltpu.make_async_copy(k_ref.at[s], k_buf.at[slot], k_sem.at[slot])

    def value_copy(s):
        slot = lax.rem(s, SLOTS)
        return pltpu.make_async_copy(v_ref.at[s], v_buf.at[slot], v_sem.at[slot])

    def peer(axis, d):
        x, y = place
        return {"sp": lax.rem(x + d, SIDE) * SIDE + y if axis == 0 else x * SIDE + lax.rem(y + d, SIDE)}

    for s in range(SLOTS):
        key_copy(s).start()
        value_copy(s).start()

    barrier = pltpu.get_barrier_semaphore()
    for axis in range(2):
        for d in range(1, SIDE):
            pl.semaphore_signal(barrier, inc=1, device_id=peer(axis, d), device_id_type=pl.DeviceIdType.MESH)

    def send(axis, c, s, count):
        mine = place[axis]
        for d in range(1, SIDE):
            for ref, s_sem, r_sem in (
                (parts.at[axis, mine, pl.ds(s, count)], send_sem, recv_sem),
                (stats.at[axis, c, mine], stat_send_sem, stat_recv_sem),
            ):
                pltpu.make_async_remote_copy(
                    src_ref=ref, dst_ref=ref, send_sem=s_sem.at[axis, c], recv_sem=r_sem.at[axis, c], device_id=peer(axis, d), device_id_type=pl.DeviceIdType.MESH
                ).start()

    def wait_all(axis, c, s, count, sem, stat_sem):
        for ref, sem in ((parts.at[axis, pl.ds(0, SIDE - 1), pl.ds(s, count)], sem), (stats.at[axis, c, pl.ds(0, SIDE - 1)], stat_sem)):
            pltpu.make_async_copy(ref, ref, sem.at[axis, c]).wait()

    def put(axis, c, s, count, sums, stat):
        for j in range(count):
            parts[axis, place[axis], s + j] = sums[j].astype(parts.dtype)
        stats[axis, c, place[axis]] = stat

    def combine(axis, c, s, count):
        wait_all(axis, c, s, count, recv_sem, stat_recv_sem)
        stat = [stats[axis, c, p] for p in range(SIDE)]
        high = functools.reduce(jnp.maximum, stat)
        weight = [jnp.exp2((t - high) * (scale * LOG2E)) for t in stat]
        total = functools.reduce(jnp.add, [a * pltpu.roll(t, 126, 1) for a, t in zip(weight, stat)])
        if axis == 1:
            weight = [w / total for w in weight]
        sums = []
        for j in range(count):
            acc = [jnp.zeros((8, head), jnp.float32)] * 2
            for p in range(SIDE):
                part = parts[axis, p, s + j].astype(jnp.float32)
                for h in range(2):
                    lane = 4 * j + h
                    acc[h] = acc[h] + part[8 * h : 8 * h + 8] * weight[p][:, lane : lane + 1]
            sums.append(jnp.concatenate(acc, 0))
        if axis == 0:
            put(1, c, s, count, sums, jnp.where(lanes % 4 < 2, high, pltpu.roll(total, 2, 1)))
        else:
            for j in range(count):
                out_ref[s + j] = sums[j].astype(out_ref.dtype)

    def attend(first, keys, values, sums, stat, base):
        for j in keys:
            key_copy(first + j).wait()
        for j in values:
            value_copy(first + j).wait()
        for j in sorted({*(j - 1 for j in keys), *values}):
            top, result, steps = [], [], []
            if j + 1 in keys:
                steps.append(score(q_ref[first + j + 1], k_buf.at[lax.rem(first + j + 1, SLOTS)], scores[(j + 1) % 2], top))
            if j in values:
                high = tops[j % 2]
                steps.append(weigh(scores[j % 2], high, v_buf.at[lax.rem(first + j, SLOTS)], scale, result))
            together(*steps)
            if top:
                tops[(j + 1) % 2] = top[0]
            if result:
                sums.append(result[0])
                for lane, value in enumerate((high[:8], high[8:16], result[1][:8], result[1][8:])):
                    stat = jnp.where(lanes == 4 * (j - base) + lane, value, stat)
        return stat

    def refill(copy, s):
        @pl.when(s < sequences)
        def _():
            copy(s).start()

    def none():
        return jnp.zeros((8, 128), jnp.float32)

    attend(0, [0], [], [], none(), 0)
    key_copy(SLOTS).start()

    @pl.loop(0, chunks - 1)
    def _(c):
        first = c * CHUNK
        sums, stat = [], none()
        for j in range(0, CHUNK, BLOCK):
            stat = attend(first, list(range(j + 1, j + BLOCK + 1)), list(range(j, j + BLOCK)), sums, stat, 0)
            for i in range(j, j + BLOCK):
                refill(key_copy, first + i + 1 + SLOTS)
                refill(value_copy, first + i + SLOTS)
        put(0, c, first, CHUNK, sums, stat)

        @pl.when(c == 0)
        def _():
            pl.semaphore_wait(barrier, 2 * (SIDE - 1))

        send(0, c, first, CHUNK)

        @pl.when(c >= 1)
        def _():
            combine(0, c - 1, first - CHUNK, CHUNK)
            send(1, c - 1, first - CHUNK, CHUNK)

        @pl.when(c >= 2)
        def _():
            combine(1, c - 2, first - 2 * CHUNK, CHUNK)

    first = sequences - CHUNK
    pieces = []
    done = 0
    for i, count in enumerate(LAST):
        sums, stat = [], none()
        for j in range(done, done + count):
            stat = attend(first, [j + 1] if j + 1 < CHUNK else [], [j], sums, stat, done)
        piece = (chunks - 1 + i, first + done, count)
        put(0, *piece, sums, stat)
        send(0, *piece)
        pieces.append(piece)
        done += count
        if i == 0:
            combine(0, chunks - 2, first - CHUNK, CHUNK)
            send(1, chunks - 2, first - CHUNK, CHUNK)
            combine(1, chunks - 3, first - 2 * CHUNK, CHUNK)
    for piece in pieces:
        combine(0, *piece)
        send(1, *piece)
    combine(1, chunks - 2, first - CHUNK, CHUNK)
    for piece in pieces:
        combine(1, *piece)

    for axis in range(2):

        @pl.loop(0, chunks - 1)
        def _(c):
            wait_all(axis, c, c * CHUNK, CHUNK, send_sem, stat_send_sem)

        for piece in pieces:
            wait_all(axis, *piece, send_sem, stat_send_sem)


def solution(mesh):
    def step(q, k, v):
        b, t, h, d = k.shape
        pieces = b // CHUNK - 1 + len(LAST)
        dma = pltpu.SemaphoreType.DMA
        return pl.pallas_call(
            functools.partial(kernel, d**-0.5),
            out_shape=jax.ShapeDtypeStruct(q.shape, q.dtype),
            in_specs=[pl.BlockSpec(memory_space=pltpu.VMEM), pl.BlockSpec(memory_space=pl.ANY), pl.BlockSpec(memory_space=pl.ANY)],
            out_specs=pl.BlockSpec(memory_space=pltpu.VMEM),
            scratch_shapes=[
                pltpu.VMEM((SLOTS, t * h, d), k.dtype),
                pltpu.VMEM((SLOTS, t * h, d), v.dtype),
                pltpu.VMEM((2 * h, t * h // 2), jnp.float32),
                pltpu.VMEM((2 * h, t * h // 2), jnp.float32),
                pltpu.VMEM((2, 2 * h, 1), jnp.float32),
                pltpu.VMEM((2, SIDE, b, h, d), jnp.bfloat16),
                pltpu.VMEM((2, pieces, SIDE, 8, 128), jnp.float32),
                dma((SLOTS,)),
                dma((SLOTS,)),
                dma((2, pieces)),
                dma((2, pieces)),
                dma((2, pieces)),
                dma((2, pieces)),
            ],
            compiler_params=pltpu.CompilerParams(collective_id=0, has_side_effects=True, vmem_limit_bytes=60 * 2**20),
        )(q, k.reshape(b, t * h, d), v.reshape(b, t * h, d))

    return jax.shard_map(
        step,
        mesh=mesh,
        in_specs=(P("dp", None, None), P("dp", "sp", None, None), P("dp", "sp", None, None)),
        out_specs=P("dp", None, None),
        check_vma=False,
    )
```

time: 168 us -> 58.4 us (0.35)
  waiting for transfers between devices: 69.3 us -> 0 us
  matrix products: 64.5 us -> 0 us
  Pallas kernels: 0 us -> 55.9 us
  other arithmetic: 15.3 us -> 0 us
  between operations: 13.5 us -> 0.01 us
  local copies, waits for them, and re-layouts: 5.22 us -> 1.57 us
    all_gather x1 -> x0, waiting for transfers between devices: 69.3 us -> none  [step(): return together(lax.all_gather(part_of(q, k, v), 'sp')).reshape(q.shape)]
    dot_general x2 -> x0, matrix products: 64.5 us -> none  [einsum(): return jnp.einsum(form, a.astype(jnp.float32), b.astype(jnp.float32))]
    pallas_call x0 -> x1, Pallas kernels: none -> 55.9 us  [step(): pl.pallas_call(functools.partial(kernel, d ** (-0.5)), out_shape=jax.Shap...]
    reduce_sum x2 -> x0, other arithmetic: 9.61 us -> none  [the longest x1 6.67 us: together(): jnp.sum(total * scale, 0)]
    mul x1 -> x0, local copies, waits for them, and re-layouts: 4.69 us -> none  [together(): seen * scale]
    reduce_max x2 -> x0, other arithmetic: 3.6 us -> none  [the longest x1 3.42 us: together(): scale = jnp.exp(high - jnp.max(high, 0))]
  transfers between devices with their start and end apart: 1 -> 0, of which waited for: 1 -> 0; matrix products, arithmetic and copies ran while one was open for 0% -> 0% of each run, Pallas kernels for 0% -> 0%
where the time goes in v2:
time: 58.4 us; the launch traced here: 57.5 us
  Pallas kernels  55.9 us (96%)
  local copies, waits for them, and re-layouts  1.57 us (3%)
    pallas_call x1, Pallas kernels, step(): pl.pallas_call(functools.partial(kernel, d ** (-0.5)), out_shape=jax.Shap...  55.9 us
    unnamed x1, local copies, waits for them, and re-layouts  1.57 us

profile of v2, /device:TPU:97, one launch (start us, length us, event | category | flops | bytes accessed | tf_op | source)
XLA Modules:
  0.0 57.5 jit_solution(6612647688935616098)
XLA Ops:
  0.0 55.9 %shard_map.37 = bf16[32,16,128]{2,1,0:T(8,128)(2,1)} custom-call(bf16[32,16,128]{2,1,0:T(8,128)(2,1)} %q_ref.1, bf16[32,8192,128]{2,1,0:T(8,128)(2,1)} %bitcast.k_ref, bf16[32,8192,128]{2,1,0:T(8,128)(2,1)} %bitcast.1.v_ref), custom_call_target="tpu_custom_call" | custom-call | tf_op jit(solution)/shard_map/pallas_call | solution.py:229
  56.0 1.6 %copy.5 = bf16[32,16,128]{2,1,0:T(8,128)(2,1)} copy(bf16[32,16,128]{2,1,0:T(8,128)(2,1)} %shard_map.37) | data formatting | bytes 262144

commit v3 on v2

v3 whole, which is shorter than its diff:
```python
import functools
import math

import jax
import jax.numpy as jnp
from jax import lax
from jax.experimental import pallas as pl
from jax.experimental.pallas import tpu as pltpu
from jax.sharding import PartitionSpec as P

SLOTS = 6
CHUNK = 4
LEAD = 2
EARLY = 3
LAG = 3
TILE = 256
LOG2E = 1.4426950408889634


def side_by_side(ref, i):
    half = ref.shape[0] // 2
    return jnp.concatenate([ref[pl.ds(i * TILE, TILE), :], ref[pl.ds(half + i * TILE, TILE), :]], 1)


def score(q, k, scores, result):
    heads = q.shape[0]
    zero = jnp.zeros_like(q)
    twice = jnp.concatenate([jnp.concatenate([q, zero], 1), jnp.concatenate([zero, q], 1)], 0)
    shape = (2 * heads, TILE)
    own = lax.broadcasted_iota(jnp.int32, shape, 0) % heads == lax.broadcasted_iota(jnp.int32, shape, 1) % heads
    high = jnp.full(shape, -jnp.inf, jnp.float32)
    for i in range(scores.shape[1] // TILE):
        s = lax.dot_general(twice, side_by_side(k, i), (((1,), (1,)), ((), ())), preferred_element_type=jnp.float32)
        s = jnp.where(own, s, -jnp.inf)
        scores[:, pl.ds(i * TILE, TILE)] = s
        high = jnp.maximum(high, s)
        yield
    result.append(high)


def weigh(scores, high, v, scale, result):
    heads, head = scores.shape[0] // 2, v.shape[1]
    top = jnp.max(high, 1, keepdims=True)
    top = jnp.maximum(top[:heads], top[heads:])
    both = jnp.concatenate([top, top], 0)
    total = jnp.zeros((2 * heads, TILE), jnp.float32)
    seen = [jnp.zeros((2 * heads, 2 * head), jnp.float32)] * 2
    for i in range(scores.shape[1] // TILE):
        w = jnp.exp2((scores[:, pl.ds(i * TILE, TILE)] - both) * (scale * LOG2E))
        total = total + w
        seen[i % 2] = seen[i % 2] + jnp.dot(w.astype(jnp.bfloat16), side_by_side(v, i), preferred_element_type=jnp.float32)
        yield
    total, seen = jnp.sum(total, 1, keepdims=True), seen[0] + seen[1]
    result.extend((seen[:heads, :head] + seen[heads:, head:], top, total[:heads] + total[heads:]))


def in_turn(steps):
    for step in steps:
        yield from step


def together(*steps):
    live = list(steps)
    while live:
        live = [s for s in live if next(s, live) is not live]


def kernel(
    side, scale, q_hbm, k_ref, v_ref, out_ref, q_ref, k_buf, v_buf, scores, tops, parts, stats, end_parts, end_stats, q_sem, k_sem, v_sem, send_sem, recv_sem, stat_send_sem, stat_recv_sem, end_sem
):
    me = lax.axis_index("sp")
    place = (lax.div(me, side), lax.rem(me, side))
    sequences, heads, head = q_ref.shape
    chunks = sequences // CHUNK
    ring = sorted(range(1, side), key=lambda d: -min(d, side - d))
    others = sorted(((dx, dy) for dx in range(side) for dy in range(side) if dx or dy), key=lambda d: -sum(min(i, side - i) for i in d))
    lanes = lax.broadcasted_iota(jnp.int32, (8, 128), 1)

    def key_copy(s):
        slot = lax.rem(s, SLOTS)
        return pltpu.make_async_copy(k_ref.at[s], k_buf.at[slot], k_sem.at[slot])

    def value_copy(s):
        slot = lax.rem(s, SLOTS)
        return pltpu.make_async_copy(v_ref.at[s], v_buf.at[slot], v_sem.at[slot])

    def peer(dx, dy):
        x, y = place
        return {"sp": lax.rem(x + dx, side) * side + lax.rem(y + dy, side)}

    q_copy = pltpu.make_async_copy(q_hbm, q_ref, q_sem)
    q_copy.start()
    for s in range(EARLY):
        key_copy(s).start()

    barrier = pltpu.get_barrier_semaphore()
    for d in others:
        pl.semaphore_signal(barrier, inc=1, device_id=peer(*d), device_id_type=pl.DeviceIdType.MESH)

    def send(axis, c, s, count):
        mine = place[axis]
        for d in ring:
            for ref, s_sem, r_sem in (
                (parts.at[axis, mine, pl.ds(s, count)], send_sem, recv_sem),
                (stats.at[axis, c, mine], stat_send_sem, stat_recv_sem),
            ):
                pltpu.make_async_remote_copy(
                    src_ref=ref, dst_ref=ref, send_sem=s_sem, recv_sem=r_sem.at[axis, c], device_id=peer(d, 0) if axis == 0 else peer(0, d), device_id_type=pl.DeviceIdType.MESH
                ).start()

    def arrive(axis, c, s, count):
        for ref, sem in ((parts.at[axis, pl.ds(0, side - 1), pl.ds(s, count)], recv_sem), (stats.at[axis, c, pl.ds(0, side - 1)], stat_recv_sem)):
            pltpu.make_async_copy(ref, ref, sem.at[axis, c]).wait()

    def put(axis, c, s, count, sums, stat):
        for j in range(count):
            parts[axis, place[axis], s + j] = sums[j].astype(parts.dtype)
        stats[axis, c, place[axis]] = stat

    def sums_of(stat, part, count, final):
        high = functools.reduce(jnp.maximum, stat)
        weight = [jnp.exp2((t - high) * (scale * LOG2E)) for t in stat]
        total = functools.reduce(jnp.add, [a * pltpu.roll(t, 126, 1) for a, t in zip(weight, stat)])
        if final:
            weight = [w / total for w in weight]
        sums = []
        for j in range(count):
            acc = [jnp.zeros((8, head), jnp.float32)] * 2
            for p, w in enumerate(weight):
                one = part(p, j).astype(jnp.float32)
                for h in range(2):
                    lane = 4 * j + h
                    acc[h] = acc[h] + one[8 * h : 8 * h + 8] * w[:, lane : lane + 1]
            sums.append(jnp.concatenate(acc, 0))
        return sums, jnp.where(lanes % 4 < 2, high, pltpu.roll(total, 2, 1))

    def combine(axis, c, s, count):
        arrive(axis, c, s, count)
        sums, stat = sums_of([stats[axis, c, p] for p in range(side)], lambda p, j: parts[axis, p, s + j], count, axis == 1)
        if axis == 0:
            put(1, c, s, count, sums, stat)
        else:
            for j in range(count):
                out_ref[s + j] = sums[j].astype(out_ref.dtype)

    def broadcast(ref, s_sem, r_sem):
        for d in others:
            pltpu.make_async_remote_copy(
                src_ref=ref, dst_ref=ref, send_sem=s_sem, recv_sem=r_sem, device_id=peer(*d), device_id_type=pl.DeviceIdType.MESH
            ).start()

    def attend(first, keys, values):
        for j in keys:
            key_copy(first + j).wait()
        for j in values:
            value_copy(first + j).wait()
        found, highs = [[] for _ in keys], [tops[j % len(scores)] for j in values]
        results = [[] for _ in values]
        together(
            in_turn([score(q_ref[first + j], k_buf.at[lax.rem(first + j, SLOTS)], scores[j % len(scores)], r) for j, r in zip(keys, found)]),
            in_turn([weigh(scores[j % len(scores)], high, v_buf.at[lax.rem(first + j, SLOTS)], scale, r) for j, high, r in zip(values, highs, results)]),
        )
        for j, (top,) in zip(keys, found):
            tops[j % len(scores)] = top
        return results

    def stat_of(rows):
        stat = jnp.zeros((8, 128), jnp.float32)
        for j, (_, high, total) in enumerate(rows):
            for lane, value in enumerate((high[:8], high[8:], total[:8], total[8:])):
                stat = jnp.where(lanes == 4 * j + lane, value, stat)
        return stat

    def refill(copy, s):
        @pl.when(s < sequences)
        def _():
            copy(s).start()

    q_copy.wait()
    for s in range(EARLY, SLOTS):
        value_copy(s - EARLY).start()
        key_copy(s).start()
    for s in range(SLOTS - EARLY, SLOTS):
        value_copy(s).start()
    for j in range(LEAD):
        attend(0, [j], [])
        key_copy(SLOTS + j).start()

    @pl.loop(0, chunks - 1)
    def _(c):
        first = c * CHUNK
        rows = []
        for j in range(CHUNK):
            rows += attend(first, [j + LEAD], [j])
            refill(key_copy, first + j + LEAD + SLOTS)
            refill(value_copy, first + j + SLOTS)
        put(0, c, first, CHUNK, [row[0] for row in rows], stat_of(rows))

        @pl.when(c == 0)
        def _():
            pl.semaphore_wait(barrier, len(others))

        send(0, c, first, CHUNK)

        @pl.when(c >= 1)
        def _():
            combine(0, c - 1, first - CHUNK, CHUNK)
            send(1, c - 1, first - CHUNK, CHUNK)

        @pl.when(c >= LAG)
        def _():
            combine(1, c - LAG, first - LAG * CHUNK, CHUNK)

    first = sequences - CHUNK
    last = (chunks - 2, first - CHUNK, CHUNK)
    rows = []
    for j in range(CHUNK):
        rows += attend(first, [j + LEAD] if j + LEAD < CHUNK else [], [j])
        end_parts[me, j] = rows[j][0].astype(end_parts.dtype)
        if j == CHUNK - 1:
            end_stats[me] = stat_of(rows)
            broadcast(end_stats.at[me], end_sem.at[1, 0], end_sem.at[1, 1])
        broadcast(end_parts.at[me, j], end_sem.at[0, 0], end_sem.at[0, 1])
    combine(0, *last)
    send(1, *last)
    for c in range(chunks - 1 - LAG, chunks - 1):
        combine(1, c, c * CHUNK, CHUNK)
    for i, ref in enumerate((end_parts, end_stats)):
        whole = ref.at[pl.ds(0, len(others))]
        pltpu.make_async_copy(whole, whole, end_sem.at[i, 1]).wait()
    sums, _ = sums_of([end_stats[p] for p in range(side * side)], lambda p, j: end_parts[p, j], CHUNK, True)
    for j in range(CHUNK):
        out_ref[first + j] = sums[j].astype(out_ref.dtype)

    for i, ref in enumerate((end_parts, end_stats)):
        whole = ref.at[pl.ds(0, len(others))]
        pltpu.make_async_copy(whole, whole, end_sem.at[i, 0]).wait()
    for ref, sem in ((parts.at[:, pl.ds(0, side - 1)], send_sem), (stats.at[:, :, pl.ds(0, side - 1)], stat_send_sem)):
        pltpu.make_async_copy(ref, ref, sem).wait()


def solution(mesh):
    side = math.isqrt(mesh.shape["sp"])

    def step(q, k, v):
        b, t, h, d = k.shape
        pieces = b // CHUNK - 1
        dma = pltpu.SemaphoreType.DMA
        return pl.pallas_call(
            functools.partial(kernel, side, d**-0.5),
            out_shape=pltpu.VMEM(q.shape, q.dtype),
            in_specs=[pl.BlockSpec(memory_space=pl.ANY)] * 3,
            out_specs=pl.BlockSpec(memory_space=pltpu.VMEM),
            scratch_shapes=[
                pltpu.VMEM((b, h, d), q.dtype),
                pltpu.VMEM((SLOTS, t * h, d), k.dtype),
                pltpu.VMEM((SLOTS, t * h, d), v.dtype),
                [pltpu.VMEM((2 * h, t * h // 2), jnp.float32)] * (2 * LEAD),
                pltpu.VMEM((2 * LEAD, 2 * h, TILE), jnp.float32),
                pltpu.VMEM((2, side, b - CHUNK, h, d), jnp.bfloat16),
                pltpu.VMEM((2, pieces, side, 8, 128), jnp.float32),
                pltpu.VMEM((side * side, CHUNK, h, d), jnp.bfloat16),
                pltpu.VMEM((side * side, 8, 128), jnp.float32),
                dma,
                dma((SLOTS,)),
                dma((SLOTS,)),
                dma,
                dma((2, pieces)),
                dma,
                dma((2, pieces)),
                dma((2, 2)),
            ],
            compiler_params=pltpu.CompilerParams(collective_id=0, has_side_effects=True, vmem_limit_bytes=60 * 2**20),
        )(q, k.reshape(b, t * h, d), v.reshape(b, t * h, d))

    return jax.shard_map(
        step,
        mesh=mesh,
        in_specs=(P("dp", None, None), P("dp", "sp", None, None), P("dp", "sp", None, None)),
        out_specs=P("dp", None, None),
        check_vma=False,
    )
```

time: 58.4 us -> 53.7 us (0.920); the launches traced: 57.5 us -> 53.6 us
  Pallas kernels: 55.9 us -> 53 us
  local copies, waits for them, and re-layouts: 1.57 us -> 0.66 us
    pallas_call x1, Pallas kernels: 55.9 us -> 53 us  [step(): pl.pallas_call(functools.partial(kernel, side, d ** (-0.5)), out_shape=pl...]
    unnamed x1, local copies, waits for them, and re-layouts: 1.57 us -> 0.66 us
where the time goes in v3:
time: 53.7 us; the launch traced here: 53.6 us
  Pallas kernels  53 us (99%)
  local copies, waits for them, and re-layouts  0.66 us (1%)
    pallas_call x1, Pallas kernels, step(): pl.pallas_call(functools.partial(kernel, side, d ** (-0.5)), out_shape=pl...  53 us

profile of v3, /device:TPU:97, one launch (start us, length us, event | category | flops | bytes accessed | tf_op | source)
XLA Modules:
  0.0 53.6 jit_solution(3834330884586046722)
XLA Ops:
  0.0 53.0 %shard_map.37 = bf16[32,16,128]{2,1,0:T(8,128)(2,1)S(1)} custom-call(bf16[32,16,128]{2,1,0:T(8,128)(2,1)} %q_hbm.1, bf16[32,8192,128]{2,1,0:T(8,128)(2,1)} %bitcast.k_ref, bf16[32,8192,128]{2,1,0:T(8,128)(2,1)} %bitcast.1.v_ref), custom_call_target="tpu_custom_call" | custom-call | tf_op jit(solution)/shard_map/pallas_call | solution.py:249
  53.0 0.7 %copy.5 = bf16[32,16,128]{2,1,0:T(8,128)(2,1)} copy(bf16[32,16,128]{2,1,0:T(8,128)(2,1)S(1)} %shard_map.37) | data formatting | bytes 262144

commit v4 on v3

--- a/solution.py
+++ b/solution.py
@@ -11,9 +11,13 @@
 SLOTS = 6
 CHUNK = 4
 LEAD = 2
+BLOCK = 1
 EARLY = 3
 LAG = 3
 TILE = 256
+END = ((0, 2), (2, 3), (3, 4))
+TAIL = END[-1][1]
+AFTER = 4
 LOG2E = 1.4426950408889634
 
 
@@ -54,6 +58,19 @@
     result.extend((seen[:heads, :head] + seen[heads:, head:], top, total[:heads] + total[heads:]))
 
 
+def sum_up(scores, high, scale, result):
+    heads = scores.shape[0] // 2
+    top = jnp.max(high, 1, keepdims=True)
+    top = jnp.maximum(top[:heads], top[heads:])
+    both = jnp.concatenate([top, top], 0)
+    total = jnp.zeros((2 * heads, TILE), jnp.float32)
+    for i in range(scores.shape[1] // TILE):
+        total = total + jnp.exp2((scores[:, pl.ds(i * TILE, TILE)] - both) * (scale * LOG2E))
+        yield
+    total = jnp.sum(total, 1, keepdims=True)
+    result.extend((top, total[:heads] + total[heads:]))
+
+
 def in_turn(steps):
     for step in steps:
         yield from step
@@ -71,7 +88,7 @@
     me = lax.axis_index("sp")
     place = (lax.div(me, side), lax.rem(me, side))
     sequences, heads, head = q_ref.shape
-    chunks = sequences // CHUNK
+    chunks = (sequences - TAIL) // CHUNK
     ring = sorted(range(1, side), key=lambda d: -min(d, side - d))
     others = sorted(((dx, dy) for dx in range(side) for dy in range(side) if dx or dy), key=lambda d: -sum(min(i, side - i) for i in d))
     lanes = lax.broadcasted_iota(jnp.int32, (8, 128), 1)
@@ -117,26 +134,27 @@
             parts[axis, place[axis], s + j] = sums[j].astype(parts.dtype)
         stats[axis, c, place[axis]] = stat
 
-    def sums_of(stat, part, count, final):
+    def weights_of(stat, final):
         high = functools.reduce(jnp.maximum, stat)
         weight = [jnp.exp2((t - high) * (scale * LOG2E)) for t in stat]
         total = functools.reduce(jnp.add, [a * pltpu.roll(t, 126, 1) for a, t in zip(weight, stat)])
         if final:
             weight = [w / total for w in weight]
-        sums = []
-        for j in range(count):
-            acc = [jnp.zeros((8, head), jnp.float32)] * 2
-            for p, w in enumerate(weight):
-                one = part(p, j).astype(jnp.float32)
-                for h in range(2):
-                    lane = 4 * j + h
-                    acc[h] = acc[h] + one[8 * h : 8 * h + 8] * w[:, lane : lane + 1]
-            sums.append(jnp.concatenate(acc, 0))
-        return sums, jnp.where(lanes % 4 < 2, high, pltpu.roll(total, 2, 1))
+        return weight, jnp.where(lanes % 4 < 2, high, pltpu.roll(total, 2, 1))
+
+    def sum_of(weight, part, j):
+        acc = [jnp.zeros((8, head), jnp.float32)] * 2
+        for p, w in enumerate(weight):
+            one = part(p).astype(jnp.float32)
+            for h in range(2):
+                lane = 4 * j + h
+                acc[h] = acc[h] + one[8 * h : 8 * h + 8] * w[:, lane : lane + 1]
+        return jnp.concatenate(acc, 0)
 
     def combine(axis, c, s, count):
         arrive(axis, c, s, count)
-        sums, stat = sums_of([stats[axis, c, p] for p in range(side)], lambda p, j: parts[axis, p, s + j], count, axis == 1)
+        weight, stat = weights_of([stats[axis, c, p] for p in range(side)], axis == 1)
+        sums = [sum_of(weight, lambda p: parts[axis, p, s + j], j) for j in range(count)]
         if axis == 0:
             put(1, c, s, count, sums, stat)
         else:
@@ -149,16 +167,23 @@
                 src_ref=ref, dst_ref=ref, send_sem=s_sem, recv_sem=r_sem, device_id=peer(*d), device_id_type=pl.DeviceIdType.MESH
             ).start()
 
-    def attend(first, keys, values):
+    def attend(first, keys, values, ahead=None):
         for j in keys:
             key_copy(first + j).wait()
         for j in values:
             value_copy(first + j).wait()
         found, highs = [[] for _ in keys], [tops[j % len(scores)] for j in values]
         results = [[] for _ in values]
-        together(
+        if ahead is not None:
+            results.append([None])
+        scoring, weighing = (
             in_turn([score(q_ref[first + j], k_buf.at[lax.rem(first + j, SLOTS)], scores[j % len(scores)], r) for j, r in zip(keys, found)]),
             in_turn([weigh(scores[j % len(scores)], high, v_buf.at[lax.rem(first + j, SLOTS)], scale, r) for j, high, r in zip(values, highs, results)]),
+        )
+        together(
+            scoring,
+            weighing,
+            sum_up(scores[ahead % len(scores)], tops[ahead % len(scores)], scale, results[-1]) if ahead is not None else iter(()),
         )
         for j, (top,) in zip(keys, found):
             tops[j % len(scores)] = top
@@ -186,15 +211,20 @@
         attend(0, [j], [])
         key_copy(SLOTS + j).start()
 
-    @pl.loop(0, chunks - 1)
+    def chunk(c, block):
+        first = c * CHUNK
+        rows = []
+        for j in range(0, CHUNK, block):
+            rows += attend(first, range(j + LEAD, j + LEAD + block), range(j, j + block))
+            for i in range(j, j + block):
+                refill(key_copy, first + i + LEAD + SLOTS)
+                refill(value_copy, first + i + SLOTS)
+        put(0, c, first, CHUNK, [row[0] for row in rows], stat_of(rows))
+
+    @pl.loop(0, chunks)
     def _(c):
         first = c * CHUNK
-        rows = []
-        for j in range(CHUNK):
-            rows += attend(first, [j + LEAD], [j])
-            refill(key_copy, first + j + LEAD + SLOTS)
-            refill(value_copy, first + j + SLOTS)
-        put(0, c, first, CHUNK, [row[0] for row in rows], stat_of(rows))
+        chunk(c, BLOCK)
 
         @pl.when(c == 0)
         def _():
@@ -211,30 +241,48 @@
         def _():
             combine(1, c - LAG, first - LAG * CHUNK, CHUNK)
 
-    first = sequences - CHUNK
-    last = (chunks - 2, first - CHUNK, CHUNK)
+    def end_whole(piece):
+        a, z = END[piece] if piece < len(END) else (0, 0)
+        return end_parts.at[pl.ds(0, len(others)), pl.ds(a, z - a)] if z else end_stats.at[pl.ds(0, len(others))]
+
+    def end_send(piece):
+        a, z = END[piece] if piece < len(END) else (0, 0)
+        broadcast(end_parts.at[me, pl.ds(a, z - a)] if z else end_stats.at[me], end_sem.at[piece, 0], end_sem.at[piece, 1])
+
+    def end_wait(piece, side):
+        whole = end_whole(piece)
+        pltpu.make_async_copy(whole, whole, end_sem.at[piece, side]).wait()
+
+    first = sequences - TAIL
     rows = []
-    for j in range(CHUNK):
-        rows += attend(first, [j + LEAD] if j + LEAD < CHUNK else [], [j])
+    for j in range(TAIL):
+        rows[j:] = attend(first, [j + LEAD] if j + LEAD < TAIL else [], [j], j + 1 if j + 2 == TAIL else None)
+        if j + LEAD + SLOTS < TAIL:
+            key_copy(first + j + LEAD + SLOTS).start()
+        if j + SLOTS < TAIL:
+            value_copy(first + j + SLOTS).start()
         end_parts[me, j] = rows[j][0].astype(end_parts.dtype)
-        if j == CHUNK - 1:
+        if j + 2 == TAIL:
             end_stats[me] = stat_of(rows)
-            broadcast(end_stats.at[me], end_sem.at[1, 0], end_sem.at[1, 1])
-        broadcast(end_parts.at[me, j], end_sem.at[0, 0], end_sem.at[0, 1])
-    combine(0, *last)
-    send(1, *last)
-    for c in range(chunks - 1 - LAG, chunks - 1):
+        if j + 1 == AFTER:
+            combine(0, chunks - 1, first - CHUNK, CHUNK)
+            send(1, chunks - 1, first - CHUNK, CHUNK)
+        for piece, (_, z) in enumerate(END):
+            if z == j + 1:
+                end_send(piece)
+        if j + 2 == TAIL:
+            end_send(len(END))
+    for c in range(chunks - LAG, chunks):
         combine(1, c, c * CHUNK, CHUNK)
-    for i, ref in enumerate((end_parts, end_stats)):
-        whole = ref.at[pl.ds(0, len(others))]
-        pltpu.make_async_copy(whole, whole, end_sem.at[i, 1]).wait()
-    sums, _ = sums_of([end_stats[p] for p in range(side * side)], lambda p, j: end_parts[p, j], CHUNK, True)
-    for j in range(CHUNK):
-        out_ref[first + j] = sums[j].astype(out_ref.dtype)
-
-    for i, ref in enumerate((end_parts, end_stats)):
-        whole = ref.at[pl.ds(0, len(others))]
-        pltpu.make_async_copy(whole, whole, end_sem.at[i, 0]).wait()
+    end_wait(len(END), 1)
+    weight, _ = weights_of([end_stats[p] for p in range(side * side)], True)
+    for piece, (a, z) in enumerate(END):
+        end_wait(piece, 1)
+        for j in range(a, z):
+            out_ref[first + j] = sum_of(weight, lambda p: end_parts[p, j], j).astype(out_ref.dtype)
+
+    for piece in range(len(END) + 1):
+        end_wait(piece, 0)
     for ref, sem in ((parts.at[:, pl.ds(0, side - 1)], send_sem), (stats.at[:, :, pl.ds(0, side - 1)], stat_send_sem)):
         pltpu.make_async_copy(ref, ref, sem).wait()
 
@@ -244,7 +292,7 @@
 
     def step(q, k, v):
         b, t, h, d = k.shape
-        pieces = b // CHUNK - 1
+        pieces = (b - TAIL) // CHUNK
         dma = pltpu.SemaphoreType.DMA
         return pl.pallas_call(
             functools.partial(kernel, side, d**-0.5),
@@ -257,9 +305,9 @@
                 pltpu.VMEM((SLOTS, t * h, d), v.dtype),
                 [pltpu.VMEM((2 * h, t * h // 2), jnp.float32)] * (2 * LEAD),
                 pltpu.VMEM((2 * LEAD, 2 * h, TILE), jnp.float32),
-                pltpu.VMEM((2, side, b - CHUNK, h, d), jnp.bfloat16),
+                pltpu.VMEM((2, side, b - TAIL, h, d), jnp.bfloat16),
                 pltpu.VMEM((2, pieces, side, 8, 128), jnp.float32),
-                pltpu.VMEM((side * side, CHUNK, h, d), jnp.bfloat16),
+                pltpu.VMEM((side * side, TAIL, h, d), jnp.bfloat16),
                 pltpu.VMEM((side * side, 8, 128), jnp.float32),
                 dma,
                 dma((SLOTS,)),
@@ -268,7 +316,7 @@
                 dma((2, pieces)),
                 dma,
                 dma((2, pieces)),
-                dma((2, 2)),
+                dma((len(END) + 1, 2)),
             ],
             compiler_params=pltpu.CompilerParams(collective_id=0, has_side_effects=True, vmem_limit_bytes=60 * 2**20),
         )(q, k.reshape(b, t * h, d), v.reshape(b, t * h, d))

time: 53.7 us -> 53.4 us (level)
  no operation moved by 1% of the time
where the time goes in v4:
time: 53.4 us; the launch traced here: 53.3 us
  Pallas kernels  52.7 us (99%)
  local copies, waits for them, and re-layouts  0.66 us (1%)
    pallas_call x1, Pallas kernels, step(): pl.pallas_call(functools.partial(kernel, side, d ** (-0.5)), out_shape=pl...  52.7 us

profile of v4, /device:TPU:97, one launch (start us, length us, event | category | flops | bytes accessed | tf_op | source)
XLA Modules:
  0.0 53.3 jit_solution(2349471397594441826)
XLA Ops:
  0.0 52.7 %shard_map.37 = bf16[32,16,128]{2,1,0:T(8,128)(2,1)S(1)} custom-call(bf16[32,16,128]{2,1,0:T(8,128)(2,1)} %q_hbm.1, bf16[32,8192,128]{2,1,0:T(8,128)(2,1)} %bitcast.k_ref, bf16[32,8192,128]{2,1,0:T(8,128)(2,1)} %bitcast.1.v_ref), custom_call_target="tpu_custom_call" | custom-call | tf_op jit(solution)/shard_map/pallas_call | solution.py:297
  52.7 0.7 %copy.5 = bf16[32,16,128]{2,1,0:T(8,128)(2,1)} copy(bf16[32,16,128]{2,1,0:T(8,128)(2,1)S(1)} %shard_map.37) | data formatting | bytes 262144
